TPU v7x, 256 devices: a 8x8x2 block of a 8x8x16 slice. The times are simulated.
256 devices in a mesh: grp: 2 (over z), row: 64 (over y, x), col: 2 (over core).
Axes of the slice: x: 8, y: 8, z: 2, core: 2. Of those that a mesh axis runs over, the one named last changes fastest.
The devices are a block of a 8x8x16 slice.
Arguments:
- factors: bfloat16 [2, 12288, 6144], P(None, ('grp', 'row'), 'col'), parts along dimension 1, may hold values from -6 to 6
- orbitals: bfloat16 [12288, 1024], P(('grp', 'row'), 'col'), parts along dimension 0, may hold values from -0.02734375 to 0.02734375
- field_term: bfloat16 [12288, 6144], P(('grp', 'row'), 'col'), parts along dimension 0, may hold values from -1.5 to 1.5
Outputs:
- fock_matrix: bfloat16 [12288, 6144], P(('grp', 'row'), 'col'), parts along dimension 0
There are 2 independent parts, one for each index of `grp`. A program takes and returns all parts, laid end to end along the dimension named above; each array names one. Nothing has to cross between parts.
All inputs are finite; a program needn't handle non-finite values.
Results may differ from a plain program's by a relative error of at most 0.02.
Values may be sent and summed in bfloat16 or wider, within the bound.
A program may use at most 64 MiB of HBM per device.

v0:
```python
import functools

import jax
import jax.numpy as jnp
from jax import lax
from jax.sharding import Mesh
from jax.sharding import PartitionSpec as P

ROW = ("row_0", "row_1")
ROW_COL = ("row_0", "row_1", "col")
GRP_ROW = ("grp", "row_0", "row_1")


def copy_for_each(value, axis):
    size = lax.axis_size(axis)
    return lax.all_to_all(
        jnp.broadcast_to(value[None], (size, *value.shape)), axis, 0, 0, tiled=True
    )


def joined_along(tiles, dim):
    tiles = jnp.moveaxis(tiles, 0, dim)
    dims = tiles.shape
    return tiles.reshape(*dims[:dim], dims[dim] * dims[dim + 1], *dims[dim + 2 :])


def collect(value, axis, dim):
    tiles = copy_for_each(value, axis)
    return joined_along(tiles, dim)


def split_up(value, dim, size):
    before, after = (value.shape[:dim], value.shape[dim + 1 :])
    return jnp.moveaxis(value.reshape(*before, size, -1, *after), dim, 0)


def sum_at_owner(value, axis, dim):
    tiles = split_up(value, dim, lax.axis_size(axis))
    arrived = lax.all_to_all(tiles, axis, split_axis=0, concat_axis=0, tiled=True)
    return arrived.astype(jnp.float32).sum(axis=0)


def by_axis(value, axes):
    return functools.reduce(lax.psum, axes, value)


def shards(factors, orbitals, field_term):
    aux_count = factors.shape[0]
    all_orbitals = lax.all_gather(orbitals, ROW, axis=0, tiled=True)
    orbit_wide = orbitals.astype(jnp.float32)
    exchange = None
    gammas = []
    for aux in range(aux_count):
        half_local = jnp.dot(
            collect(factors[aux], "col", 1), all_orbitals, preferred_element_type=jnp.float32
        ).astype(jnp.bfloat16)
        local_fit = jnp.sum(half_local.astype(jnp.float32) * orbit_wide)
        gammas.append(local_fit)
        term = lax.dot_general(
            half_local,
            lax.all_gather(half_local, ROW, axis=0, tiled=True),
            (((1,), (1,)), ((), ())),
            preferred_element_type=jnp.float32,
        )
        reduced = sum_at_owner(term.astype(jnp.bfloat16), "col", 1)
        exchange = reduced if exchange is None else exchange + reduced
    fitted = by_axis(jnp.stack(gammas), ROW_COL)
    gammas = [fitted[aux] for aux in range(aux_count)]
    coulomb = jnp.zeros(field_term.shape, jnp.float32)
    for aux in range(aux_count):
        coulomb = coulomb + gammas[aux] * factors[aux].astype(jnp.float32)
    fock_matrix = field_term.astype(jnp.float32) + coulomb - 0.25 * exchange
    return fock_matrix.astype(jnp.bfloat16)


def solution(mesh):
    finer = Mesh(
        mesh.devices.reshape(mesh.shape["grp"], 8, 8, mesh.shape["col"]),
        ("grp", "row_0", "row_1", "col"),
    )
    return jax.shard_map(
        shards,
        mesh=finer,
        in_specs=(P(None, GRP_ROW, "col"), P(GRP_ROW, "col"), P(GRP_ROW, "col")),
        out_specs=P(GRP_ROW, "col"),
        check_vma=False,
    )
```

profile of v0, /device:TPU:513, one launch (start us, length us, event | category | flops | bytes accessed | tf_op | source)
XLA Modules:
  0.0 318.9 jit_solution(6659823777059124831)
XLA Ops:
  6.5 0.0 all-gather.4.cloned.1.call-start
  6.6 0.7 all-gather.4.cloned.1.call-update
  7.3 1.3 slice_bitcast_fusion
  8.6 0.1 broadcast_in_dim.17
  8.8 24.7 %all_to_all.20 = bf16[2,96,3072]{2,1,0:T(8,128)(2,1)S(1)} all-to-all(bf16[2,96,3072]{2,1,0:T(8,128)(2,1)S(1)} %broadcast_in_dim.17), channel_id=1, replica_groups=mesh['grp'=2,'row_0'=8,'row_1'=8,'col'=2] {'col'}, dimensions={0} | all-to-all | bytes 2359296 | tf_op jit(solution)/shard_map/all_to_all | solution.py:16
  33.5 1.2 broadcast_in_dim.15
  34.7 4.0 %all-to-all-start = ((bf16[2,96,3072]{2,1,0:T(8,128)(2,1)}), bf16[2,96,3072]{2,1,0:T(8,128)(2,1)S(1)}, u32[]{:S(2)}, u32[]{:S(2)}) async-start(bf16[2,96,3072]{2,1,0:T(8,128)(2,1)} %broadcast_in_dim.15), calls=%async_computation | async-start | bytes 2359296 | tf_op jit(solution)/shard_map/all_to_all | solution.py:16
  38.7 0.0 all-gather.6.cloned.1.call-start
  38.7 0.1 copy.11
  38.8 1.7 all-to-all-done
  40.5 0.1 copy.10
  40.6 73.8 %all-gather.4.cloned.1.call-done = bf16[6144,512]{1,0:T(8,128)(2,1)} async-done(((bf16[96,512]{1,0:T(8,128)(2,1)}), bf16[6144,512]{1,0:T(8,128)(2,1)}) %all-gather.4.cloned.1.call-update) | async-done | bytes 6291472 | tf_op jit(solution)/shard_map/all_gather | solution.py:49
  114.3 0.0 copy-start.4
  114.4 3.9 %convolution_convert_fusion.2 = bf16[96,512]{1,0:T(8,128)(2,1)S(1)} fusion(bf16[96,6144]{1,0:T(8,128)(2,1)S(1)} %bitcast.45, bf16[6144,512]{1,0:T(8,128)(2,1)} %all-gather.4.cloned.1.call-done), kind=kOutput, calls=%fused_computation.7 | convolution fusion | flops 604028928 | bytes 7569408 | tf_op jit(solution)/shard_map/dot_general | solution.py:54
  118.3 0.0 copy-start.1
  118.3 0.0 copy-done.4
  118.3 5.2 %fusion = (f32[]{:T(128)}, f32[]{:T(128)}, bf16[96,512]{1,0:T(8,128)(2,1)}) fusion(bf16[96,512]{1,0:T(8,128)(2,1)S(1)} %copy-done.4, bf16[96,512]{1,0:T(8,128)(2,1)S(1)} %convolution_convert_fusion.2, bf16[96,6144]{1,0:T(8,128)(2,1)S(1)} %bitcast.42, bf16[6144,512]{1,0:T(8,128)(2,1)} %all-gather.4.cloned.1.call-done), kind=kOutput, calls=%fused_computation.13 | convolution fusion | flops 604372992 | bytes 7766024 | tf_op jit(solution)/shard_map/dot_general | solution.py:54
  123.5 0.0 copy-done.1
  123.5 0.1 all-gather.6.cloned.1.call-update
  123.6 0.1 all-gather.8.cloned.1.call-start
  123.7 0.7 all-gather.8.cloned.1.call-update
  124.4 1.2 pad_maximum_fusion
  125.6 12.1 %psum.21 = f32[2]{0:T(128)S(1)} all-reduce(f32[2]{0:T(128)S(1)} %pad_maximum_fusion), channel_id=1, replica_groups=mesh['grp'=2,'row_0'=8,'row_1'=8,'col'=2] {'row_0'}, use_global_device_ids=true, to_apply=%region_2.0 | all-reduce | flops 2 | bytes 16 | tf_op jit(solution)/shard_map/psum | solution.py:44
  137.7 12.8 %psum.22 = f32[2]{0:T(128)S(1)} all-reduce(f32[2]{0:T(128)S(1)} %psum.21), channel_id=1, replica_groups=mesh['grp'=2,'row_0'=8,'row_1'=8,'col'=2] {'row_1'}, use_global_device_ids=true, to_apply=%region_3.0 | all-reduce | flops 2 | bytes 16 | tf_op jit(solution)/shard_map/psum | solution.py:44
  150.5 11.3 %psum.23 = f32[2]{0:T(128)S(1)} all-reduce(f32[2]{0:T(128)S(1)} %psum.22), channel_id=1, replica_groups=mesh['grp'=2,'row_0'=8,'row_1'=8,'col'=2] {'col'}, use_global_device_ids=true, to_apply=%region_4.0 | all-reduce | flops 2 | bytes 16 | tf_op jit(solution)/shard_map/psum | solution.py:44
  161.8 0.6 fusion.2
  162.4 45.8 %all-gather.6.cloned.1.call-done = bf16[6144,512]{1,0:T(8,128)(2,1)} async-done(((bf16[96,512]{1,0:T(8,128)(2,1)}), bf16[6144,512]{1,0:T(8,128)(2,1)}) %all-gather.6.cloned.1.call-update) | async-done | bytes 6291472 | tf_op jit(solution)/shard_map/all_gather | solution.py:61
  208.2 4.8 %convolution_convert_fusion.1 = bf16[96,6144]{1,0:T(8,128)(2,1)S(1)} fusion(bf16[96,512]{1,0:T(8,128)(2,1)} %get-tuple-element.11, bf16[6144,512]{1,0:T(8,128)(2,1)} %all-gather.6.cloned.1.call-done), kind=kOutput, calls=%fused_computation.1 | convolution fusion | flops 604569600 | bytes 7569408 | tf_op jit(solution)/shard_map/dot_general | solution.py:59
  213.1 1.1 copy.15
  214.2 0.0 copy-start.2
  214.2 6.1 %all-to-all-start.2 = ((bf16[2,96,3072]{2,1,0:T(8,128)(2,1)}), bf16[2,96,3072]{2,1,0:T(8,128)(2,1)S(1)}, u32[]{:S(2)}, u32[]{:S(2)}) async-start(bf16[2,96,3072]{2,1,0:T(8,128)(2,1)} %bitcast.39), calls=%async_computation.2 | async-start | bytes 2359296 | tf_op jit(solution)/shard_map/all_to_all | solution.py:39
  220.2 74.9 %all-gather.8.cloned.1.call-done = bf16[6144,512]{1,0:T(8,128)(2,1)} async-done(((bf16[96,512]{1,0:T(8,128)(2,1)}), bf16[6144,512]{1,0:T(8,128)(2,1)}) %all-gather.8.cloned.1.call-update) | async-done | bytes 6291472 | tf_op jit(solution)/shard_map/all_gather | solution.py:61
  295.2 0.0 copy-done.2
  295.2 4.8 %convolution_convert_fusion = bf16[96,6144]{1,0:T(8,128)(2,1)S(1)} fusion(bf16[96,512]{1,0:T(8,128)(2,1)S(1)} %copy-done.2, bf16[6144,512]{1,0:T(8,128)(2,1)} %all-gather.8.cloned.1.call-done), kind=kOutput, calls=%fused_computation | convolution fusion | flops 604569600 | bytes 7569408 | tf_op jit(solution)/shard_map/dot_general | solution.py:59
  300.0 1.1 copy.14
  301.1 0.0 all-to-all-done.2
  301.1 5.9 %all-to-all-start.3 = ((bf16[2,96,3072]{2,1,0:T(8,128)(2,1)}), bf16[2,96,3072]{2,1,0:T(8,128)(2,1)S(1)}, u32[]{:S(2)}, u32[]{:S(2)}) async-start(bf16[2,96,3072]{2,1,0:T(8,128)(2,1)} %bitcast.37), calls=%async_computation.3 | async-start | bytes 2359296 | tf_op jit(solution)/shard_map/all_to_all | solution.py:39
  307.0 0.2 convert_reduce_fusion.1
  307.2 0.0 copy-start
  307.2 1.6 all-to-all-done.3
  308.8 0.0 copy-start.3
  308.8 0.2 convert_reduce_fusion
  309.1 0.0 copy-done
  309.1 0.8 copy-done.3
  309.9 2.4 subtract_convert_fusion
Async XLA Ops:
  6.5 107.8 %all-gather.4.cloned.1.call-start = ((), (), s32[]{:S(2)}) async-start(), calls=%async_computation.4 | async-start | bytes 6389760 | tf_op jit(solution)/shard_map/all_gather | solution.py:49
  34.7 5.8 %all-to-all-start = ((bf16[2,96,3072]{2,1,0:T(8,128)(2,1)}), bf16[2,96,3072]{2,1,0:T(8,128)(2,1)S(1)}, u32[]{:S(2)}, u32[]{:S(2)}) async-start(bf16[2,96,3072]{2,1,0:T(8,128)(2,1)} %broadcast_in_dim.15), calls=%async_computation | async-start | bytes 2359296 | tf_op jit(solution)/shard_map/all_to_all | solution.py:16
  38.7 169.6 %all-gather.6.cloned.1.call-start = ((), (), s32[]{:S(2)}) async-start(), calls=%async_computation.5 | async-start | bytes 6389760 | tf_op jit(solution)/shard_map/all_gather | solution.py:61
  114.3 4.0 %copy-start.4 = (bf16[96,512]{1,0:T(8,128)(2,1)S(1)}, bf16[96,512]{1,0:T(8,128)(2,1)}, u32[]{:S(2)}) copy-start(bf16[96,512]{1,0:T(8,128)(2,1)} %param.4) | copy-start | bytes 294916
  118.3 5.2 %copy-start.1 = (bf16[96,512]{1,0:T(8,128)(2,1)}, bf16[96,512]{1,0:T(8,128)(2,1)S(1)}, u32[]{:S(2)}) copy-start(bf16[96,512]{1,0:T(8,128)(2,1)S(1)} %convolution_convert_fusion.2) | copy-start | bytes 294916
  123.6 171.6 %all-gather.8.cloned.1.call-start = ((), (), s32[]{:S(2)}) async-start(), calls=%async_computation.6 | async-start | bytes 6389760 | tf_op jit(solution)/shard_map/all_gather | solution.py:61
  214.2 81.0 %copy-start.2 = (bf16[96,512]{1,0:T(8,128)(2,1)S(1)}, bf16[96,512]{1,0:T(8,128)(2,1)}, u32[]{:S(2)}) copy-start(bf16[96,512]{1,0:T(8,128)(2,1)} %copy-done.1) | copy-start | bytes 294916
  214.2 86.9 %all-to-all-start.2 = ((bf16[2,96,3072]{2,1,0:T(8,128)(2,1)}), bf16[2,96,3072]{2,1,0:T(8,128)(2,1)S(1)}, u32[]{:S(2)}, u32[]{:S(2)}) async-start(bf16[2,96,3072]{2,1,0:T(8,128)(2,1)} %bitcast.39), calls=%async_computation.2 | async-start | bytes 2359296 | tf_op jit(solution)/shard_map/all_to_all | solution.py:39
  301.1 7.8 %all-to-all-start.3 = ((bf16[2,96,3072]{2,1,0:T(8,128)(2,1)}), bf16[2,96,3072]{2,1,0:T(8,128)(2,1)S(1)}, u32[]{:S(2)}, u32[]{:S(2)}) async-start(bf16[2,96,3072]{2,1,0:T(8,128)(2,1)} %bitcast.37), calls=%async_computation.3 | async-start | bytes 2359296 | tf_op jit(solution)/shard_map/all_to_all | solution.py:39
  307.2 1.8 copy-start
  308.8 1.1 copy-start.3
Sparse Core Ops, SparseCore 0:
  9.8 104.4 all-gather.3
  123.7 84.4 all-gather.5
  210.7 84.4 all-gather.7
where the time goes:
time: 320 us; the launch traced here: 319 us
  waiting for transfers between devices  199 us (62%)
  blocking collectives  60.9 us (19%)
  matrix products  18.8 us (6%)
  starting transfers between devices  16 us (5%)
  between operations  13.2 us (4%)
  local copies, waits for them, and re-layouts  6.48 us (2%)
  other arithmetic  4.08 us (1%)
    all_gather x2, waiting for transfers between devices, shards(): lax.all_gather(half_local, ROW, axis=0, tiled=True)  121 us
    all_gather x1, waiting for transfers between devices, shards(): all_orbitals = lax.all_gather(orbitals, ROW, axis=0, tiled=True)  73.8 us
    psum x3, blocking collectives, by_axis(): return functools.reduce(lax.psum, axes, value)  36.1 us
    all_to_all x1, blocking collectives, copy_for_each(): lax.all_to_all(jnp.broadcast_to(value[None], (size, *value.shape)), axis,...  24.7 us
    all_to_all x2, starting transfers between devices, sum_at_owner(): lax.all_to_all(tiles, axis, split_axis=0, concat_axis=0, tiled=True)  12 us
    dot_general x2, matrix products, shards(): lax.dot_general(half_local, lax.all_gather(half_local, ROW, axis=0, tiled...  9.64 us
    dot_general x2, matrix products, shards(): jnp.dot(collect(factors[aux], 'col', 1), all_orbitals, preferred_element_...  9.15 us
  transfers between devices with their start and end apart: 6, of which 5 were waited for; matrix products, arithmetic and copies ran while one was open for 5% of the time, Pallas kernels for 0%

commit v1 on v0

v1 whole, which is shorter than its diff:
```python
import functools
import math

import jax
import jax.numpy as jnp
from jax import lax
from jax.experimental import pallas as pl
from jax.experimental.pallas import tpu as pltpu
from jax.sharding import Mesh
from jax.sharding import PartitionSpec as P

GRP_ROW = ("grp", "row_0", "row_1")
AXES = ("row_1", "row_0")
LANES = 128


def offset_of(unit):
    return ((unit + 1) // 2) * (2 * (unit % 2) - 1)


def fock_kernel(
    side, f_hbm, c_hbm, t_hbm, o_hbm,
    bfull, blocal, call, hacc, rbuf, cbuf, ksx, ksy, krecv, field, base, out, gx, gy, gd,
    loc, osem, bsem, s1s, s1r, s2s, s2r, hs, hr, ds_, dr, xs, ys, kr, gxs, gxr, gys, gyr, gds, gdr,
):
    naux, n, ncol = f_hbm.shape
    ni = c_hbm.shape[1]
    w = ni // 2
    far = side // 2
    y, x, c = (lax.axis_index(a) for a in ("row_0", "row_1", "col"))
    pos = (x, y)
    sib = {"col": 1 - c}

    def at(p, off):
        return lax.rem(p + (off + side), side)

    def neighbour(axis, off):
        return {AXES[axis]: at(pos[axis], off)}

    def remote(src, dst, ssem, rsem, device):
        return pltpu.make_async_remote_copy(
            src_ref=src, dst_ref=dst, send_sem=ssem, recv_sem=rsem,
            device_id=device, device_id_type=pl.DeviceIdType.MESH,
        )

    def rows(k, d):
        if k < far:
            return pl.ds(0, n)
        return pl.ds(0, n // 2) if d > 0 else pl.ds(n // 2, n // 2)

    my_slot = y * side + x
    own_c = [
        pltpu.make_async_copy(c_hbm.at[:, pl.ds(h * w, w)], call.at[h, my_slot], loc.at[h])
        for h in range(2)
    ]
    half_cols = pl.ds(pl.multiple_of(c * ncol, LANES), ncol)
    own_b = pltpu.make_async_copy(f_hbm, bfull.at[:, :, half_cols], loc.at[2])
    own_b2 = pltpu.make_async_copy(f_hbm, blocal, loc.at[3])
    own_t = pltpu.make_async_copy(t_hbm, field, loc.at[4])
    for copy in (*own_c, own_b, own_b2, own_t):
        copy.start()
    barrier = pltpu.get_barrier_semaphore()

    def hello(device):
        pl.semaphore_signal(
            barrier, inc=1, device_id=device, device_id_type=pl.DeviceIdType.MESH
        )

    hello(sib)
    for off in range(1, side):
        hello(neighbour(0, off))
        hello(neighbour(1, off))
        hello({**neighbour(1, off), **sib})
    pl.semaphore_wait(barrier, 3 * (side - 1) + 1)

    def slot(h, off1, off2):
        if h == 0:
            return at(y, off2) * side + at(x, off1)
        return at(y, off1) * side + at(x, off2)

    def s1(h, k, d, off):
        ref = call.at[h, slot(h, off, 0), rows(k, d)]
        i = (h, (1 - d) // 2, k - 1)
        return remote(ref, ref, s1s.at[i], s1r.at[i], neighbour(h, d))

    def s2(h, k, d, unit, off):
        ref = call.at[h, slot(h, offset_of(unit), off), rows(k, d)]
        di = (1 - d) // 2
        return remote(
            ref, ref, s2s.at[h, di, k - 1, unit], s2r.at[h, di, k - 1, unit], neighbour(1 - h, d)
        )

    both = [(h, d) for h in range(2) for d in (1, -1)]
    for copy in own_c:
        copy.wait()
    for h, d in both:
        s1(h, 1, d, 0).start()
    for h, d in both:
        s2(h, 1, d, 0, 0).start()
    own_b.wait()
    mine = bfull.at[:, :, half_cols]
    swap_b = remote(mine, mine, bsem.at[0], bsem.at[1], sib)
    swap_b.start()
    for k in range(1, far + 1):
        for h, d in both:
            s1(h, k, d, -k * d).wait_recv()
            if k < far:
                s1(h, k + 1, d, -k * d).start()
                unit = 2 * k if d > 0 else 2 * k - 1
                for e in (1, -1):
                    s2(h, 1, e, unit, 0).start()
            elif d < 0:
                for e in (1, -1):
                    s2(h, 1, e, 2 * k - 1, 0).start()
    for k in range(1, far + 1):

        def hop(unit, carry, k=k):
            for h, d in both:
                s2(h, k, d, unit, -k * d).wait_recv()
                if k < far:
                    s2(h, k + 1, d, unit, -k * d).start()
            return carry

        lax.fori_loop(0, side, hop, 0)

    theirs = bfull.at[:, :, pl.ds(pl.multiple_of((1 - c) * ncol, LANES), ncol)]
    remote(theirs, theirs, bsem.at[0], bsem.at[1], sib).wait_recv()
    hacc[...] = jnp.zeros_like(hacc)
    deep = side * n

    @pl.loop(0, side)
    def _(i):
        left = bfull[:, :, pl.ds(pl.multiple_of(i * deep, LANES), deep)].reshape(naux * n, deep)
        for h in range(2):
            right = call[h, pl.ds(i * side, side)].reshape(deep, w)
            hacc[h] += jnp.dot(left, right, preferred_element_type=jnp.float32)

    sums = [jnp.zeros((1, 1), jnp.float32) for _ in range(naux)]
    for h in range(2):
        own = call[h, my_slot].astype(jnp.float32)
        for p in range(naux):
            block = hacc[h, pl.ds(p * n, n), :].astype(jnp.bfloat16)
            lanes = pl.ds(p * ni + h * w, w)
            rbuf[c, x, pl.ds(0, n), lanes] = block
            cbuf[c, y, pl.ds(0, n), lanes] = block
            sums[p] += jnp.sum(block.astype(jnp.float32) * own, keepdims=True)

    bufs = (rbuf, cbuf)
    units = 2 * naux

    def lanes_of(u):
        h, p = divmod(u, naux)
        return pl.ds(p * ni + h * w, w)

    def ring(a, k, d, u, off):
        ref = bufs[a].at[c, at(pos[a], off), rows(k, d), lanes_of(u)]
        i = (a, (1 - d) // 2, k - 1, u)
        return remote(ref, ref, hs.at[i], hr.at[i], neighbour(a, d))

    def share(a, off, u, core):
        ref = bufs[a].at[core, at(pos[a], off), pl.ds(0, n), lanes_of(u)]
        i = (a, off % side, u)
        return remote(ref, ref, ds_.at[i], dr.at[i], sib)

    for u in range(units):
        for a, d in both:
            ring(a, 1, d, u, 0).start()
    for u in range(units):
        for a in range(2):
            share(a, 0, u, c).start()

    line = lax.broadcasted_iota(jnp.int32, (8, LANES), 0)
    tile = jnp.zeros((8, LANES), jnp.float32)
    for p in range(naux):
        tile = jnp.where(line == p, sums[p], tile)
    gx[x] = tile

    def gamma_copy(a, off):
        buf, ss, rs = ((gx, gxs, gxr), (gy, gys, gyr))[a]
        return remote(buf.at[pos[a]], buf.at[pos[a]], ss.at[off - 1], rs.at[off - 1], neighbour(a, off))

    def gamma_wait(a, off):
        buf, ss, rs = ((gx, gxs, gxr), (gy, gys, gyr))[a]
        ref = buf.at[at(pos[a], -off)]
        remote(ref, ref, ss.at[off - 1], rs.at[off - 1], neighbour(a, off)).wait_recv()

    for off in range(1, side):
        gamma_copy(0, off).start()

    for k in range(1, far + 1):
        for u in range(units):
            for a, d in both:
                ring(a, k, d, u, -k * d).wait_recv()
                if k < far:
                    ring(a, k + 1, d, u, -k * d).start()
                    share(a, -k * d, u, c).start()
                elif d < 0:
                    share(a, far, u, c).start()
        if k == 2:
            for off in range(1, side):
                gamma_wait(0, off)
            gy[y] = jnp.sum(gx[...], axis=0)
            for off in range(1, side):
                gamma_copy(1, off).start()
    for off in range(1, side):
        gamma_wait(1, off)
    gd[c] = jnp.sum(gy[...], axis=0)
    swap_g = remote(gd.at[c], gd.at[c], gds, gdr, sib)
    swap_g.start()
    for a in range(2):
        for off in range(side):
            for u in range(units):
                share(a, off, u, 1 - c).wait_recv()

    deep = naux * ni
    first = c * far
    nt = (((1,), (1,)), ((), ()))

    def by_x(target_x, block_y):
        return along_x(at(x, -target_x), at(block_y, -y))

    def along_x(dx, dy):
        a, b = jnp.minimum(dx, side - dx), jnp.minimum(dy, side - dy)
        return (a < b) | ((a == b) & ((dx < far) == (dy < far)))

    def send_x(q, i):
        return remote(
            ksx.at[q, i], krecv.at[q, x], xs.at[q, i], kr.at[q, x], {"row_1": i}
        )

    def x_sent(q, i):
        return (i != x) & (first + q != y) & by_x(i, first + q)

    y_half = y // far

    def send_y(q, i):
        there = lax.rem(y, far)
        return remote(
            ksy.at[q, i], krecv.at[there, i], ys.at[q, i], kr.at[there, i],
            {"row_0": first + q, "col": y_half},
        )

    def y_sent(q, i):
        return (i != x) & (first + q != y) & jnp.logical_not(
            along_x(at(i, -x), at(y, -(first + q)))
        )

    for j in range(far // 2):
        acc = None
        for core in range(2):
            left = rbuf[core, :, pl.ds(0, n), :].reshape(side * n, deep)
            right = cbuf[core, pl.ds(first + 2 * j, 2)].reshape(2 * LANES, deep)
            term = lax.dot_general(left, right, nt, preferred_element_type=jnp.float32)
            acc = term if acc is None else acc + term
        for i in range(2):
            ksx[2 * j + i] = (
                acc[:, i * LANES : (i + 1) * LANES].astype(jnp.bfloat16).reshape(side, n, LANES)
            )
        for i in range(2):

            @pl.loop(0, side)
            def _(t, q=2 * j + i):
                pl.when(x_sent(q, t))(lambda: send_x(q, t).start())

    for j in range(side // 2):
        acc = None
        for core in range(2):
            left = cbuf[core, pl.ds(first, far), pl.ds(0, n), :].reshape(far * n, deep)
            right = rbuf[core, pl.ds(2 * j, 2)].reshape(2 * LANES, deep)
            term = lax.dot_general(left, right, nt, preferred_element_type=jnp.float32)
            acc = term if acc is None else acc + term
        for i in range(2):
            part = acc[:, i * LANES : (i + 1) * LANES].astype(jnp.bfloat16).reshape(far, n, LANES)
            ksy[:, 2 * j + i] = part
        for i in range(2):

            @pl.loop(0, far)
            def _(q, t=2 * j + i):
                pl.when(y_sent(q, t))(lambda: send_y(q, t).start())

    for q in range(far):
        krecv[q, x] = ksx[q, x]

        @pl.when(first + q == y)
        def _(q=q):
            @pl.loop(0, side)
            def _(i):
                @pl.when(i != x)
                def _():
                    krecv[q, i] = ksy[q, i]

    own_b2.wait()
    own_t.wait()
    other = gd.at[1 - c]
    remote(other, other, gds, gdr, sib).wait_recv()
    gamma = jnp.sum(gd[...], axis=0)
    width = side * n

    @pl.loop(0, far)
    def _(q):
        cols = pl.ds(pl.multiple_of(q * width, LANES), width)
        total = field[:, cols].astype(jnp.float32)
        for p in range(naux):
            total += gamma[p : p + 1, 0:1] * blocal[p, :, cols].astype(jnp.float32)
        base[:, cols] = total

    lane = lax.broadcasted_iota(jnp.int32, (n, LANES), 1)
    for q in range(far):

        @pl.loop(0, side)
        def _(i, q=q):
            @pl.when((i != x) & (first + q != y))
            def _():
                ref = krecv.at[q, i]
                remote(ref, ref, xs.at[q, i], kr.at[q, i], sib).wait_recv()

        for g in range(side // 4):
            b = [krecv[q, 4 * g + i].astype(jnp.float32) for i in range(4)]
            r = [b[0]] + [pltpu.roll(b[i], LANES - 32 * i, 1) for i in range(1, 4)]
            for t in range(3):
                start = q * width + g * 4 * n + t * LANES
                cols = pl.ds(start, LANES)
                piece = jnp.where(lane < n - 32 * t, r[t], r[t + 1])
                out[:, cols] = (base[:, cols] - 0.25 * piece).astype(out.dtype)
        cols = pl.ds(q * width, width)
        pltpu.make_async_copy(out.at[:, cols], o_hbm.at[:, cols], osem.at[q]).start()

    for k in range(1, far + 1):
        for h, d in both:
            s1(h, k, d, -(k - 1) * d).wait_send()

        def sent(unit, carry, k=k):
            for h, d in both:
                s2(h, k, d, unit, -(k - 1) * d).wait_send()
            return carry

        lax.fori_loop(0, side, sent, 0)
        for u in range(units):
            for a, d in both:
                ring(a, k, d, u, -(k - 1) * d).wait_send()
    swap_b.wait_send()
    swap_g.wait_send()
    for off in range(1, side):
        gamma_copy(0, off).wait_send()
        gamma_copy(1, off).wait_send()
    for a in range(2):
        for off in range(side):
            for u in range(units):
                share(a, off, u, c).wait_send()
    for q in range(far):

        @pl.loop(0, side)
        def _(i, q=q):
            pl.when(x_sent(q, i))(lambda: send_x(q, i).wait_send())
            pl.when(y_sent(q, i))(lambda: send_y(q, i).wait_send())

    for q in range(far):
        cols = pl.ds(q * width, width)
        pltpu.make_async_copy(out.at[:, cols], o_hbm.at[:, cols], osem.at[q]).wait()


def shards(side, factors, orbitals, field_term):
    naux, n, ncol = factors.shape
    ni = orbitals.shape[1]
    w = ni // 2
    far = side // 2
    units = 2 * naux
    bf16, f32, dma = jnp.bfloat16, jnp.float32, pltpu.SemaphoreType.DMA
    hbm = pl.BlockSpec(memory_space=pl.ANY)
    return pl.pallas_call(
        functools.partial(fock_kernel, side),
        out_shape=jax.ShapeDtypeStruct((n, ncol), bf16),
        in_specs=[hbm] * 3,
        out_specs=hbm,
        scratch_shapes=[
            pltpu.VMEM((naux, n, 2 * ncol), bf16),
            pltpu.VMEM((naux, n, ncol), bf16),
            pltpu.VMEM((2, side * side, n, w), bf16),
            pltpu.VMEM((2, naux * n, w), f32),
            pltpu.VMEM((2, side, LANES, naux * ni), bf16),
            pltpu.VMEM((2, side, LANES, naux * ni), bf16),
            pltpu.VMEM((far, side, n, LANES), bf16),
            pltpu.VMEM((far, side, n, LANES), bf16),
            pltpu.VMEM((far, side, n, LANES), bf16),
            pltpu.VMEM((n, ncol), bf16),
            pltpu.VMEM((n, ncol), f32),
            pltpu.VMEM((n, ncol), bf16),
            pltpu.VMEM((side, 8, LANES), f32),
            pltpu.VMEM((side, 8, LANES), f32),
            pltpu.VMEM((2, 8, LANES), f32),
            dma((5,)),
            dma((far,)),
            dma((2,)),
            dma((2, 2, far)),
            dma((2, 2, far)),
            dma((2, 2, far, side)),
            dma((2, 2, far, side)),
            dma((2, 2, far, units)),
            dma((2, 2, far, units)),
            dma((2, side, units)),
            dma((2, side, units)),
            dma((far, side)),
            dma((far, side)),
            dma((far, side)),
            dma((side - 1,)),
            dma((side - 1,)),
            dma((side - 1,)),
            dma((side - 1,)),
            dma,
            dma,
        ],
        compiler_params=pltpu.CompilerParams(
            collective_id=0, has_side_effects=True, vmem_limit_bytes=60 * 1024 * 1024
        ),
        name="fock",
    )(factors, orbitals, field_term)


def solution(mesh):
    side = math.isqrt(mesh.shape["row"])
    finer = Mesh(
        mesh.devices.reshape(mesh.shape["grp"], side, side, mesh.shape["col"]),
        ("grp", "row_0", "row_1", "col"),
    )
    return jax.shard_map(
        functools.partial(shards, side),
        mesh=finer,
        in_specs=(P(None, GRP_ROW, "col"), P(GRP_ROW, "col"), P(GRP_ROW, "col")),
        out_specs=P(GRP_ROW, "col"),
        check_vma=False,
    )
```

time: 320 us -> 108 us (0.34)
  waiting for transfers between devices: 199 us -> 0 us
  Pallas kernels: 0 us -> 106 us
  blocking collectives: 60.9 us -> 0 us
  matrix products: 18.8 us -> 0 us
  starting transfers between devices: 16 us -> 0 us
  between operations: 13.2 us -> 0.01 us
  local copies, waits for them, and re-layouts: 6.48 us -> 1.92 us
  other arithmetic: 4.08 us -> 0 us
    all_gather x3 -> x0, waiting for transfers between devices: 195 us -> none  [the longest x2 121 us: shards(): lax.all_gather(half_local, ROW, axis=0, tiled=True)]
    pallas_call x0 -> x1, Pallas kernels: none -> 106 us  [shards(): pl.pallas_call(functools.partial(fock_kernel, side), out_shape=jax.ShapeD...]
    psum x3 -> x0, blocking collectives: 36.1 us -> none  [by_axis(): return functools.reduce(lax.psum, axes, value)]
    all_to_all x1 -> x0, blocking collectives: 24.7 us -> none  [copy_for_each(): lax.all_to_all(jnp.broadcast_to(value[None], (size, *value.shape)), axis,...]
    dot_general x4 -> x0, matrix products: 18.8 us -> none  [the longest x2 9.64 us: shards(): lax.dot_general(half_local, lax.all_gather(half_local, ROW, axis=0, tiled...]
    all_to_all x3 -> x0, starting transfers between devices: 16 us -> none  [the longest x2 12 us: sum_at_owner(): lax.all_to_all(tiles, axis, split_axis=0, concat_axis=0, tiled=True)]
    all_to_all x3 -> x0, waiting for transfers between devices: 3.37 us -> none  [the longest x1 1.74 us: copy_for_each(): lax.all_to_all(jnp.broadcast_to(value[None], (size, *value.shape)), axis,...]
  transfers between devices with their start and end apart: 6 -> 0, of which waited for: 5 -> 0; matrix products, arithmetic and copies ran while one was open for 5% -> 0% of each run, Pallas kernels for 0% -> 0%
where the time goes in v1:
time: 108 us
  Pallas kernels  106 us (98%)
  local copies, waits for them, and re-layouts  1.92 us (2%)
    pallas_call x1, Pallas kernels, shards(): pl.pallas_call(functools.partial(fock_kernel, side), out_shape=jax.ShapeD...  106 us

profile of v1, /device:TPU:513, one launch (start us, length us, event | category | flops | bytes accessed | tf_op | source)
XLA Modules:
  0.0 108.3 jit_solution(852328426977627820)
XLA Ops:
  0.0 106.4 %fock.1 = bf16[96,3072]{1,0:T(8,128)(2,1)} custom-call(bf16[2,96,3072]{2,1,0:T(8,128)(2,1)} %f_hbm.1, bf16[96,512]{1,0:T(8,128)(2,1)} %c_hbm.1, bf16[96,3072]{1,0:T(8,128)(2,1)} %t_hbm.1), custom_call_target="tpu_custom_call" | custom-call | tf_op jit(solution)/shard_map/fock/pallas_call | solution.py:370
  106.4 1.9 %copy.5 = bf16[96,3072]{1,0:T(8,128)(2,1)} copy(bf16[96,3072]{1,0:T(8,128)(2,1)} %fock.1) | data formatting | bytes 1179648

commit v2 on v0

v2 whole, which is shorter than its diff:
```python
import functools
import math

import jax
import jax.numpy as jnp
from jax import lax
from jax.experimental import pallas as pl
from jax.experimental.pallas import tpu as pltpu
from jax.sharding import Mesh
from jax.sharding import PartitionSpec as P

GRP_ROW = ("grp", "row_0", "row_1")
AXES = ("row_1", "row_0")
LANES = 128
CHUNKS = 2


def offset_of(unit):
    return ((unit + 1) // 2) * (2 * (unit % 2) - 1)


def fock_kernel(
    side, chunks, f_hbm, c_hbm, t_hbm, o_hbm,
    bfull, blocal, call, hacc, rbuf, cbuf, kxacc, kyacc, ksx, ksy, krx, kry, field, base, out, gx, gy, gd,
    loc, osem, bsem, s1s, s1r, s2s, s2r, hs, hr, ds_, dr, xs, ys, krxs, krys, gxs, gxr, gys, gyr, gds, gdr,
):
    naux, n, ncol = f_hbm.shape
    ni = c_hbm.shape[1]
    wide = ni // chunks
    w = wide // 2
    far = side // 2
    near = far // 2
    y, x, c = (lax.axis_index(a) for a in ("row_0", "row_1", "col"))
    pos = (x, y)
    sib = {"col": 1 - c}

    def at(p, off):
        return lax.rem(p + (off + side), side)

    def neighbour(axis, off):
        return {AXES[axis]: at(pos[axis], off)}

    def remote(src, dst, ssem, rsem, device):
        return pltpu.make_async_remote_copy(
            src_ref=src, dst_ref=dst, send_sem=ssem, recv_sem=rsem,
            device_id=device, device_id_type=pl.DeviceIdType.MESH,
        )

    def rows(k, d):
        if k < far:
            return pl.ds(0, n)
        return pl.ds(0, n // 2) if d > 0 else pl.ds(n // 2, n // 2)

    my_slot = y * side + x
    own_c = [
        pltpu.make_async_copy(c_hbm.at[:, pl.ds(q * wide, wide)], call.at[q, my_slot], loc.at[q])
        for q in range(chunks)
    ]
    half_cols = pl.ds(pl.multiple_of(c * ncol, LANES), ncol)
    own_b = pltpu.make_async_copy(f_hbm, bfull.at[:, :, half_cols], loc.at[chunks])
    own_b2 = pltpu.make_async_copy(f_hbm, blocal, loc.at[chunks + 1])
    own_t = pltpu.make_async_copy(t_hbm, field, loc.at[chunks + 2])
    for copy in (*own_c, own_b, own_b2, own_t):
        copy.start()
    barrier = pltpu.get_barrier_semaphore()
    friends = [sib] + [neighbour(axis, off) for axis in range(2) for off in (1, -1)]
    for device in friends:
        pl.semaphore_signal(
            barrier, inc=1, device_id=device, device_id_type=pl.DeviceIdType.MESH
        )
    pl.semaphore_wait(barrier, len(friends))

    both = [(h, d) for h in range(2) for d in (1, -1)]

    def slot(h, off1, off2):
        if h == 0:
            return at(y, off2) * side + at(x, off1)
        return at(y, off1) * side + at(x, off2)

    def s1(q, h, k, d, off):
        ref = call.at[q, slot(h, off, 0), rows(k, d), pl.ds(h * w, w)]
        i = (q, h, (1 - d) // 2, k - 1)
        return remote(ref, ref, s1s.at[i], s1r.at[i], neighbour(h, d))

    def s2(q, h, k, d, unit, off):
        ref = call.at[q, slot(h, offset_of(unit), off), rows(k, d), pl.ds(h * w, w)]
        i = (q, h, (1 - d) // 2, k - 1, unit)
        return remote(ref, ref, s2s.at[i], s2r.at[i], neighbour(1 - h, d))

    def begin(q):
        own_c[q].wait()
        for h, d in both:
            s1(q, h, 1, d, 0).start()
        for h, d in both:
            s2(q, h, 1, d, 0, 0).start()

    def first_hop(q, k):
        for h, d in both:
            s1(q, h, k, d, -k * d).wait_recv()
            if k < far:
                s1(q, h, k + 1, d, -k * d).start()
                unit = 2 * k if d > 0 else 2 * k - 1
                for e in (1, -1):
                    s2(q, h, 1, e, unit, 0).start()
            elif d < 0:
                for e in (1, -1):
                    s2(q, h, 1, e, 2 * k - 1, 0).start()

    def second_hop(q, k):
        def hop(unit, carry):
            for h, d in both:
                s2(q, h, k, d, unit, -k * d).wait_recv()
                if k < far:
                    s2(q, h, k + 1, d, unit, -k * d).start()
            return carry

        lax.fori_loop(0, side, hop, 0)

    deep = side * n
    sums = [jnp.zeros((1, 1), jnp.float32) for _ in range(naux)]

    def lanes_of(q, p):
        return pl.ds((q * naux + p) * wide, wide)

    def half_transform(q):
        hacc[...] = jnp.zeros_like(hacc)

        @pl.loop(0, side)
        def _(i):
            left = bfull[:, :, pl.ds(pl.multiple_of(i * deep, LANES), deep)]
            right = call[q, pl.ds(i * side, side)].reshape(deep, wide)
            hacc[...] += jnp.dot(
                left.reshape(naux * n, deep), right, preferred_element_type=jnp.float32
            )

        own = call[q, my_slot].astype(jnp.float32)
        for p in range(naux):
            block = hacc[pl.ds(p * n, n), :].astype(jnp.bfloat16)
            rbuf[c, x, :, lanes_of(q, p)] = block
            cbuf[c, near, pl.ds(0, n), lanes_of(q, p)] = block
            sums[p] += jnp.sum(block.astype(jnp.float32) * own, keepdims=True)

    units = 2 * naux

    def part(a, core, off, rs, q, u):
        lanes = pl.ds((q * units + u) * w, w)
        if a == 0:
            return rbuf.at[core, at(x, off), rs, lanes]
        return cbuf.at[core, (off + near) % side, rs, lanes]

    def ring(q, a, k, d, u):
        i = (q, a, (1 - d) // 2, k - 1, u)
        src = part(a, c, -(k - 1) * d, rows(k, d), q, u)
        dst = src if a == 0 else part(a, c, -k * d, rows(k, d), q, u)
        return remote(src, dst, hs.at[i], hr.at[i], neighbour(a, d))

    def ring_in(q, a, k, d, u):
        i = (q, a, (1 - d) // 2, k - 1, u)
        ref = part(a, c, -k * d, rows(k, d), q, u)
        return remote(ref, ref, hs.at[i], hr.at[i], neighbour(a, d))

    def share(q, a, off, u, core):
        ref = part(a, core, off, pl.ds(0, n), q, u)
        i = (q, a, off % side, u)
        return remote(ref, ref, ds_.at[i], dr.at[i], sib)

    def begin_ring(q):
        for u in range(units):
            for a, d in both:
                ring(q, a, 1, d, u).start()
        for u in range(units):
            for a in range(2):
                share(q, a, 0, u, c).start()

    def ring_hop(q, k):
        for u in range(units):
            for a, d in both:
                ring_in(q, a, k, d, u).wait_recv()
                if k < far:
                    ring(q, a, k + 1, d, u).start()
                    share(q, a, -k * d, u, c).start()
                elif d < 0:
                    share(q, a, far, u, c).start()

    def shared(q):
        for a in range(2):
            for off in range(side):
                for u in range(units):
                    share(q, a, off, u, 1 - c).wait_recv()

    first = c * far
    nt = (((1,), (1,)), ((), ()))
    band = 2 * near + 1
    rest = side - band

    def products(q):
        lanes = pl.ds(q * naux * wide, naux * wide)
        span = naux * wide
        kx = ky = None
        for core in range(2):
            ours = rbuf[core, pl.ds(first, far), :, lanes].reshape(far * n, span)
            close = cbuf[core, pl.ds(0, band), pl.ds(0, n), lanes].reshape(band * n, span)
            away = cbuf[core, pl.ds(band, rest), :, lanes].reshape(rest * LANES, span)
            tx = lax.dot_general(ours, away, nt, preferred_element_type=jnp.float32)
            ty = lax.dot_general(close, ours, nt, preferred_element_type=jnp.float32)
            kx = tx if kx is None else kx + tx
            ky = ty if ky is None else ky + ty
        return kx, ky

    gammas = ((gx, gxs, gxr), (gy, gys, gyr))

    def gamma_copy(a, off):
        buf, ss, rs = gammas[a]
        ref = buf.at[pos[a]]
        return remote(ref, ref, ss.at[off - 1], rs.at[off - 1], neighbour(a, off))

    def gamma_wait(a, off):
        buf, ss, rs = gammas[a]
        ref = buf.at[at(pos[a], -off)]
        remote(ref, ref, ss.at[off - 1], rs.at[off - 1], neighbour(a, off)).wait_recv()

    swap_g = remote(gd.at[c], gd.at[c], gds, gdr, sib)

    mine = bfull.at[:, :, half_cols]
    theirs = bfull.at[:, :, pl.ds(pl.multiple_of((1 - c) * ncol, LANES), ncol)]
    swap_b = remote(mine, mine, bsem.at[0], bsem.at[1], sib)

    begin(0)
    own_b.wait()
    swap_b.start()
    for k in range(1, far + 1):
        first_hop(0, k)
    remote(theirs, theirs, bsem.at[0], bsem.at[1], sib).wait_recv()
    last = chunks - 1
    for q in range(chunks):
        if q < last:
            begin(q + 1)
        for k in range(1, far + 1):
            second_hop(q, k)
            if q > 0:
                ring_hop(q - 1, k)
            if q < last:
                first_hop(q + 1, k)
        half_transform(q)
        begin_ring(q)
        if q > 0:
            shared(q - 1)
            kx, ky = products(q - 1)
            if q > 1:
                kx, ky = kxacc[...] + kx, kyacc[...] + ky
            kxacc[...] = kx
            kyacc[...] = ky

    line = lax.broadcasted_iota(jnp.int32, (8, LANES), 0)
    tile = jnp.zeros((8, LANES), jnp.float32)
    for p in range(naux):
        tile = jnp.where(line == p, sums[p], tile)
    gx[x] = tile
    for off in range(1, side):
        gamma_copy(0, off).start()
    for k in range(1, far + 1):
        ring_hop(last, k)
        if k == 2:
            for off in range(1, side):
                gamma_wait(0, off)
            gy[y] = jnp.sum(gx[...], axis=0)
            for off in range(1, side):
                gamma_copy(1, off).start()
    for off in range(1, side):
        gamma_wait(1, off)
    gd[c] = jnp.sum(gy[...], axis=0)
    swap_g.start()
    shared(last)
    kx, ky = products(last)
    if last > 0:
        kx, ky = kxacc[...] + kx, kyacc[...] + ky

    y_half = y // far
    y_low = lax.rem(y, far)

    def x_block(j):
        other = at(y, near + 1 + j)
        return other // far, lax.rem(other, far)

    def send_x(j, i):
        core, low = x_block(j)
        return remote(
            ksx.at[j, i], krx.at[low, x], xs.at[j, i], krxs.at[low, x],
            {"row_1": first + i, "col": core},
        )

    def x_stays(j, i):
        core, _ = x_block(j)
        return (first + i == x) & (core == c)

    def send_y(m):
        return remote(
            ksy.at[m], kry.at[y_low, c], ys.at[m], krys.at[y_low, c],
            {"row_0": at(y, m - near), "col": y_half},
        )

    y_stays = y_half == c
    for j in range(rest):
        piece = kx[:, j * LANES : (j + 1) * LANES].astype(jnp.bfloat16)
        ksx[j] = piece.reshape(far, n, LANES)
        for i in range(far):
            pl.when(jnp.logical_not(x_stays(j, i)))(lambda j=j, i=i: send_x(j, i).start())
    ksy[...] = ky.astype(jnp.bfloat16).reshape(band, n, far * n)
    for m in range(band):
        if m == near:
            pl.when(jnp.logical_not(y_stays))(lambda m=m: send_y(m).start())
        else:
            send_y(m).start()

    for j in range(rest):
        for i in range(far):

            @pl.when(x_stays(j, i))
            def _(j=j, i=i):
                krx[x_block(j)[1], x] = ksx[j, i]

    @pl.when(y_stays)
    def _():
        kry[y_low, c] = ksy[near]

    own_b2.wait()
    own_t.wait()
    other = gd.at[1 - c]
    remote(other, other, gds, gdr, sib).wait_recv()
    gamma = jnp.sum(gd[...], axis=0)
    width = side * n

    @pl.loop(0, far)
    def _(q):
        cols = pl.ds(pl.multiple_of(q * width, LANES), width)
        total = field[:, cols].astype(jnp.float32)
        for p in range(naux):
            total += gamma[p : p + 1, 0:1] * blocal[p, :, cols].astype(jnp.float32)
        base[:, cols] = total

    lane = lax.broadcasted_iota(jnp.int32, (n, LANES), 1)
    for q in range(far):
        dy = at(first + q, -y)
        by_x = (dy > near) & (dy < side - near)

        @pl.when(by_x)
        def _(q=q):
            @pl.loop(0, side)
            def _(i):
                @pl.when((i != x) | (x // far != c))
                def _():
                    ref = krx.at[q, i]
                    remote(ref, ref, xs.at[0, 0], krxs.at[q, i], sib).wait_recv()

            for g in range(side // 4):
                b = [krx[q, 4 * g + i].astype(jnp.float32) for i in range(4)]
                r = [b[0]] + [pltpu.roll(b[i], LANES - 32 * i, 1) for i in range(1, 4)]
                for t in range(3):
                    cols = pl.ds(q * width + g * 4 * n + t * LANES, LANES)
                    piece = jnp.where(lane < n - 32 * t, r[t], r[t + 1])
                    out[:, cols] = (base[:, cols] - 0.25 * piece).astype(out.dtype)

        @pl.when(jnp.logical_not(by_x))
        def _(q=q, dy=dy):
            for g in range(2):

                @pl.when((dy != 0) | (c != g))
                def _(g=g):
                    ref = kry.at[q, g]
                    remote(ref, ref, ys.at[0], krys.at[q, g], sib).wait_recv()

                cols = pl.ds(q * width + g * far * n, far * n)
                piece = kry[q, g].astype(jnp.float32)
                out[:, cols] = (base[:, cols] - 0.25 * piece).astype(out.dtype)

        cols = pl.ds(q * width, width)
        pltpu.make_async_copy(out.at[:, cols], o_hbm.at[:, cols], osem.at[q]).start()

    for q in range(chunks):
        for k in range(1, far + 1):
            for h, d in both:
                s1(q, h, k, d, -(k - 1) * d).wait_send()

            def sent(unit, carry, q=q, k=k):
                for h, d in both:
                    s2(q, h, k, d, unit, -(k - 1) * d).wait_send()
                return carry

            lax.fori_loop(0, side, sent, 0)
            for u in range(units):
                for a, d in both:
                    ring(q, a, k, d, u).wait_send()
        for a in range(2):
            for off in range(side):
                for u in range(units):
                    share(q, a, off, u, c).wait_send()
    swap_b.wait_send()
    swap_g.wait_send()
    for off in range(1, side):
        gamma_copy(0, off).wait_send()
        gamma_copy(1, off).wait_send()
    for j in range(rest):
        for i in range(far):
            pl.when(jnp.logical_not(x_stays(j, i)))(lambda j=j, i=i: send_x(j, i).wait_send())
    for m in range(band):
        if m == near:
            pl.when(jnp.logical_not(y_stays))(lambda m=m: send_y(m).wait_send())
        else:
            send_y(m).wait_send()
    for q in range(far):
        cols = pl.ds(q * width, width)
        pltpu.make_async_copy(out.at[:, cols], o_hbm.at[:, cols], osem.at[q]).wait()


def shards(side, chunks, factors, orbitals, field_term):
    naux, n, ncol = factors.shape
    ni = orbitals.shape[1]
    wide = ni // chunks
    far = side // 2
    band = 2 * (far // 2) + 1
    rest = side - band
    units = 2 * naux
    bf16, f32, dma = jnp.bfloat16, jnp.float32, pltpu.SemaphoreType.DMA
    hbm = pl.BlockSpec(memory_space=pl.ANY)
    return pl.pallas_call(
        functools.partial(fock_kernel, side, chunks),
        out_shape=jax.ShapeDtypeStruct((n, ncol), bf16),
        in_specs=[hbm] * 3,
        out_specs=hbm,
        scratch_shapes=[
            pltpu.VMEM((naux, n, 2 * ncol), bf16),
            pltpu.VMEM((naux, n, ncol), bf16),
            pltpu.VMEM((chunks, side * side, n, wide), bf16),
            pltpu.VMEM((naux * n, wide), f32),
            pltpu.VMEM((2, side, n, naux * ni), bf16),
            pltpu.VMEM((2, side, LANES, naux * ni), bf16),
            pltpu.VMEM((far * n, rest * LANES), f32),
            pltpu.VMEM((band * n, far * n), f32),
            pltpu.VMEM((rest, far, n, LANES), bf16),
            pltpu.VMEM((band, n, far * n), bf16),
            pltpu.VMEM((far, side, n, LANES), bf16),
            pltpu.VMEM((far, 2, n, far * n), bf16),
            pltpu.VMEM((n, ncol), bf16),
            pltpu.VMEM((n, ncol), f32),
            pltpu.VMEM((n, ncol), bf16),
            pltpu.VMEM((side, 8, LANES), f32),
            pltpu.VMEM((side, 8, LANES), f32),
            pltpu.VMEM((2, 8, LANES), f32),
            dma((chunks + 3,)),
            dma((far,)),
            dma((2,)),
            dma((chunks, 2, 2, far)),
            dma((chunks, 2, 2, far)),
            dma((chunks, 2, 2, far, side)),
            dma((chunks, 2, 2, far, side)),
            dma((chunks, 2, 2, far, units)),
            dma((chunks, 2, 2, far, units)),
            dma((chunks, 2, side, units)),
            dma((chunks, 2, side, units)),
            dma((rest, far)),
            dma((band,)),
            dma((far, side)),
            dma((far, 2)),
            dma((side - 1,)),
            dma((side - 1,)),
            dma((side - 1,)),
            dma((side - 1,)),
            dma,
            dma,
        ],
        compiler_params=pltpu.CompilerParams(
            collective_id=0, has_side_effects=True, vmem_limit_bytes=60 * 1024 * 1024
        ),
        name="fock",
    )(factors, orbitals, field_term)


def solution(mesh):
    side = math.isqrt(mesh.shape["row"])
    finer = Mesh(
        mesh.devices.reshape(mesh.shape["grp"], side, side, mesh.shape["col"]),
        ("grp", "row_0", "row_1", "col"),
    )
    return jax.shard_map(
        functools.partial(shards, side, CHUNKS),
        mesh=finer,
        in_specs=(P(None, GRP_ROW, "col"), P(GRP_ROW, "col"), P(GRP_ROW, "col")),
        out_specs=P(GRP_ROW, "col"),
        check_vma=False,
    )
```

time: 320 us -> 113 us (0.35)
  waiting for transfers between devices: 199 us -> 0 us
  Pallas kernels: 0 us -> 111 us
  blocking collectives: 60.9 us -> 0 us
  matrix products: 18.8 us -> 0 us
  starting transfers between devices: 16 us -> 0 us
  between operations: 13.2 us -> 0.01 us
  local copies, waits for them, and re-layouts: 6.48 us -> 1.92 us
  other arithmetic: 4.08 us -> 0 us
    all_gather x3 -> x0, waiting for transfers between devices: 195 us -> none  [the longest x2 121 us: shards(): lax.all_gather(half_local, ROW, axis=0, tiled=True)]
    pallas_call x0 -> x1, Pallas kernels: none -> 111 us  [shards(): pl.pallas_call(functools.partial(fock_kernel, side, chunks), out_shape=ja...]
    psum x3 -> x0, blocking collectives: 36.1 us -> none  [by_axis(): return functools.reduce(lax.psum, axes, value)]
    all_to_all x1 -> x0, blocking collectives: 24.7 us -> none  [copy_for_each(): lax.all_to_all(jnp.broadcast_to(value[None], (size, *value.shape)), axis,...]
    dot_general x4 -> x0, matrix products: 18.8 us -> none  [the longest x2 9.64 us: shards(): lax.dot_general(half_local, lax.all_gather(half_local, ROW, axis=0, tiled...]
    all_to_all x3 -> x0, starting transfers between devices: 16 us -> none  [the longest x2 12 us: sum_at_owner(): lax.all_to_all(tiles, axis, split_axis=0, concat_axis=0, tiled=True)]
    all_to_all x3 -> x0, waiting for transfers between devices: 3.37 us -> none  [the longest x1 1.74 us: copy_for_each(): lax.all_to_all(jnp.broadcast_to(value[None], (size, *value.shape)), axis,...]
  transfers between devices with their start and end apart: 6 -> 0, of which waited for: 5 -> 0; matrix products, arithmetic and copies ran while one was open for 5% -> 0% of each run, Pallas kernels for 0% -> 0%
where the time goes in v2:
time: 113 us
  Pallas kernels  111 us (98%)
  local copies, waits for them, and re-layouts  1.92 us (2%)
    pallas_call x1, Pallas kernels, shards(): pl.pallas_call(functools.partial(fock_kernel, side, chunks), out_shape=ja...  111 us

profile of v2, /device:TPU:513, one launch (start us, length us, event | category | flops | bytes accessed | tf_op | source)
XLA Modules:
  0.0 112.7 jit_solution(10986964828483898480)
XLA Ops:
  0.0 110.8 %fock.1 = bf16[96,3072]{1,0:T(8,128)(2,1)} custom-call(bf16[2,96,3072]{2,1,0:T(8,128)(2,1)} %f_hbm.1, bf16[96,512]{1,0:T(8,128)(2,1)} %c_hbm.1, bf16[96,3072]{1,0:T(8,128)(2,1)} %t_hbm.1), custom_call_target="tpu_custom_call" | custom-call | tf_op jit(solution)/shard_map/fock/pallas_call | solution.py:425
  110.8 1.9 %copy.5 = bf16[96,3072]{1,0:T(8,128)(2,1)} copy(bf16[96,3072]{1,0:T(8,128)(2,1)} %fock.1) | data formatting | bytes 1179648
